TPU v7x, 32 devices: a 4x4x1 block of a 4x4x8 slice. The times are simulated.
32 devices in a mesh: rep: 2 (over z, core), dp: 16 (over x, y).
Axes of the slice: x: 4, y: 4, z: 1, core: 2. Of those that a mesh axis runs over, the one named last changes fastest.
The devices are a block of a 4x4x8 slice.
Arguments:
- x: bfloat16 [32, 2048, 768], P(('rep', 'dp')), parts along dimension 0
- dy: bfloat16 [32, 2048, 768], P(('rep', 'dp')), parts along dimension 0
- w_gate: bfloat16 [2, 768, 2304], replicated
- w_up: bfloat16 [2, 768, 2304], replicated
- w_down: bfloat16 [2, 2304, 768], replicated
- m_w_gate: float32 [2, 768, 2304], replicated
- m_w_up: float32 [2, 768, 2304], replicated
- m_w_down: float32 [2, 2304, 768], replicated
- v_w_gate: float32 [2, 768, 2304], replicated
- v_w_up: float32 [2, 768, 2304], replicated
- v_w_down: float32 [2, 2304, 768], replicated
Outputs:
- output 1: bfloat16 [4, 768, 2304], P('rep'), parts along dimension 0
- output 2: bfloat16 [4, 768, 2304], P('rep'), parts along dimension 0
- output 3: bfloat16 [4, 2304, 768], P('rep'), parts along dimension 0
- output 4: float32 [4, 768, 2304], P('rep'), parts along dimension 0
- output 5: float32 [4, 768, 2304], P('rep'), parts along dimension 0
- output 6: float32 [4, 2304, 768], P('rep'), parts along dimension 0
- output 7: float32 [4, 768, 2304], P('rep'), parts along dimension 0
- output 8: float32 [4, 768, 2304], P('rep'), parts along dimension 0
- output 9: float32 [4, 2304, 768], P('rep'), parts along dimension 0
There are 2 independent parts. A program takes and returns all parts, laid end to end along the dimension named above; an argument that names none is the same for every part.
All inputs are finite; a program needn't handle non-finite values.
Results may differ from a plain program's by a relative error of at most 0.022.
Values are sent between devices in bfloat16 or wider.
A program may use at most 768 MiB of HBM per device.

v0:
```python
import jax
import jax.numpy as jnp
from jax import lax
from jax.sharding import PartitionSpec as P

NAMES = ("w_gate", "w_up", "w_down")


def matmul(a, w):
    return jnp.dot(a, w, preferred_element_type=jnp.float32).astype(jnp.bfloat16)


def normed(h):
    wide = h.astype(jnp.float32)
    scale = lax.rsqrt(jnp.mean(wide**2, -1, keepdims=True) + 1e-6)
    return (wide * scale).astype(jnp.bfloat16)


def layer(h, w):
    a = normed(h)
    gate = jnp.dot(a, w["w_gate"], preferred_element_type=jnp.float32)
    up = jnp.dot(a, w["w_up"], preferred_element_type=jnp.float32)
    return h + matmul((jax.nn.silu(gate) * up).astype(jnp.bfloat16), w["w_down"])


def adamw(w, m, v, g):
    m = 0.9 * m + 0.1 * g
    v = 0.95 * v + 0.05 * g * g
    step = m * lax.rsqrt(v + 1e-8) + 0.1 * w
    return (w - 0.02 * step).astype(jnp.bfloat16), m, v


def clipped(gradients, sum_of_squares, count):
    factor = jnp.minimum(1.0, 0.5 * lax.rsqrt(sum_of_squares / count + 1e-30))
    return [g * factor for g in gradients]


def solution(mesh):
    def step(x, dy, *arrays):
        weights, m, v = (arrays[i : i + 3] for i in (0, 3, 6))
        layers = weights[0].shape[0]
        h, kept = x[0], []
        for number in range(layers):
            kept.append(h)
            h = layer(h, {name: w[number] for name, w in zip(NAMES, weights, strict=True)})
        by_h, summed = dy[0], [None] * layers
        for number in reversed(range(layers)):
            _, back = jax.vjp(lambda w, h: layer(h, w), {name: w[number] for name, w in zip(NAMES, weights, strict=True)}, kept[number])
            by_w, by_h = back(by_h)
            summed[number] = [lax.psum(by_w[name], "dp") for name in NAMES]
        gradients = [jnp.stack([summed[number][i] for number in range(layers)]).astype(jnp.float32) for i in range(3)]
        gradients = clipped(gradients, sum(jnp.sum(g * g) for g in gradients), sum(g.size for g in gradients))
        new = [adamw(w.astype(jnp.float32), m, v, g) for w, m, v, g in zip(weights, m, v, gradients, strict=True)]
        return tuple(one[which] for which in range(3) for one in new)

    return jax.shard_map(
        step,
        mesh=mesh,
        in_specs=(P(("rep", "dp"), None, None),) * 2 + (P(None, None, None),) * 9,
        out_specs=(P("rep", None, None),) * 9,
        check_vma=False,
    )
```

profile of v0, /device:TPU:97, one launch (start us, length us, event | category | flops | bytes accessed | tf_op | source)
XLA Modules:
  0.0 614.8 jit_solution(13110440119602132647)
XLA Ops:
  7.2 0.1 all-reduce.3.cloned.1.call-start
  7.3 3.2 copy.20
  10.5 0.0 copy-start.2
  10.5 0.7 fusion.36
  11.2 5.0 copy.21
  16.2 12.5 %convolution_convert_fusion.1 = bf16[2048,2304]{1,0:T(8,128)(2,1)} fusion(bf16[2,2304,768]{2,1,0:T(8,128)(2,1)} %param.15, bf16[1,2048,768]{2,1,0:T(8,128)(2,1)} %param.12), kind=kOutput, calls=%fused_computation.59 | convolution fusion | flops 7252475904 | bytes 16121856 | tf_op jit(solution)/shard_map/transpose(jvp())/dot_general | solution.py:10
  28.7 13.0 %fusion.70 = f32[2048,2304]{1,0:T(8,128)} fusion(bf16[2,768,2304]{2,1,0:T(8,128)(2,1)} %param.13, bf16[1,2048,768]{2,1,0:T(8,128)(2,1)S(1)} %copy-done.5, f32[2048]{0:T(1024)S(1)} %add_rsqrt_fusion), kind=kOutput, calls=%fused_computation.105 | convolution fusion | flops 7252475904 | bytes 25567232 | tf_op jit(solution)/shard_map/dot_general | solution.py:21
  41.7 19.0 %multiply_convert_fusion.1 = (bf16[2048,2304]{1,0:T(8,128)(2,1)}, f32[2048,2304]{1,0:T(8,128)}) fusion(f32[2048,2304]{1,0:T(8,128)} %fusion.70, bf16[2,768,2304]{2,1,0:T(8,128)(2,1)} %param.14, bf16[1,2048,768]{2,1,0:T(8,128)(2,1)} %param.11, f32[2048]{0:T(1024)S(1)} %add_rsqrt_fusion), kind=kOutput, calls=%fused_computation.20 | convolution fusion | flops 7280787456 | bytes 53878784 | tf_op jit(solution)/shard_map/dot_general | solution.py:22
  60.7 11.9 %fusion.40 = (f32[2048]{0:T(1024)S(1)}, bf16[2048,768]{0,1:T(8,128)(2,1)S(1)}) fusion(bf16[2048,2304]{1,0:T(8,128)(2,1)} %get-tuple-element.24, bf16[2,2304,768]{2,1,0:T(8,128)(2,1)} %param.15, bf16[1,2048,768]{1,2,0:T(8,128)(2,1)S(1)} %copy.20), kind=kOutput, calls=%fused_computation.76 | convolution fusion | flops 7255619584 | bytes 19275776 | tf_op jit(solution)/shard_map/dot_general | solution.py:10
  72.6 0.6 copy-done.9
  73.1 1.1 copy-done.7
  74.2 13.5 %fusion.57 = f32[2048,2304]{1,0:T(8,128)} fusion(bf16[2,768,2304]{2,1,0:T(8,128)(2,1)} %param.14, bf16[2048,768]{0,1:T(8,128)(2,1)S(1)} %get-tuple-element.27, f32[2048]{0:T(1024)S(1)} %fusion.108), kind=kOutput, calls=%fused_computation.92 | convolution fusion | flops 7252475904 | bytes 25567232 | tf_op jit(solution)/shard_map/jvp()/dot_general | solution.py:22
  87.8 30.5 %fusion.2 = (bf16[2048,2304]{1,0:T(8,128)(2,1)}, f32[2048,2304]{1,0:T(8,128)}) fusion(f32[2048,2304]{1,0:T(8,128)} %fusion.57, bf16[2048,2304]{1,0:T(8,128)(2,1)} %convolution_convert_fusion.1, bf16[2,768,2304]{2,1,0:T(8,128)(2,1)} %param.13, bf16[2048,768]{0,1:T(8,128)(2,1)} %copy-done.7, f32[2048]{0:T(1024)S(1)} %fusion.108), kind=kOutput, calls=%fused_computation.11 | convolution fusion | flops 7309099008 | bytes 63315968 | tf_op jit(solution)/shard_map/jvp()/dot_general | solution.py:21
  118.3 11.3 %fusion.78 = bf16[2048,768]{0,1:T(8,128)(2,1)} fusion(bf16[2048,2304]{1,0:T(8,128)(2,1)} %get-tuple-element.28, bf16[2,768,2304]{2,1,0:T(8,128)(2,1)S(1)} %bitcast.83), kind=kOutput, calls=%fused_computation.111 | convolution fusion | flops 7247757312 | bytes 16121856 | tf_op jit(solution)/shard_map/transpose(jvp())/dot_general | solution.py:21
  129.7 8.9 %fusion.50 = bf16[1,768,2304]{2,1,0:T(8,128)(2,1)} fusion(bf16[2048,2304]{1,0:T(8,128)(2,1)S(1)} %copy-done.13, bf16[2048,768]{0,1:T(8,128)(2,1)S(1)} %copy-done.8, f32[2048]{0:T(1024)S(1)} %fusion.108), kind=kOutput, calls=%fused_computation.87 | convolution fusion | flops 7252475904 | bytes 16130048 | tf_op jit(solution)/shard_map/transpose(jvp())/dot_general | solution.py:21
  138.6 18.0 %fusion.49 = bf16[1,2304,768]{2,1,0:T(8,128)(2,1)} fusion(f32[2048,2304]{1,0:T(8,128)} %fusion.57, bf16[1,2048,768]{2,1,0:T(8,128)(2,1)S(1)} %copy-done.6, f32[2048,2304]{1,0:T(8,128)} %get-tuple-element.29), kind=kOutput, calls=%fused_computation.86 | convolution fusion | flops 7277838336 | bytes 44433408 | tf_op jit(solution)/shard_map/transpose(jvp())/dot_general | solution.py:10
  156.6 16.4 %fusion.56 = bf16[1,768,2304]{2,1,0:T(8,128)(2,1)} fusion(bf16[2048,2304]{1,0:T(8,128)(2,1)} %convolution_convert_fusion.1, bf16[2048,768]{0,1:T(8,128)(2,1)} %copy-done.7, f32[2048]{0:T(1024)S(1)} %fusion.108, f32[2048,2304]{1,0:T(8,128)} %get-tuple-element.29), kind=kOutput, calls=%fused_computation.91 | convolution fusion | flops 7282556928 | bytes 35004416 | tf_op jit(solution)/shard_map/transpose(jvp())/dot_general | solution.py:22
  173.0 19.6 %fusion.42 = (f32[2048]{0:T(1024)S(1)}, bf16[2048,768]{0,1:T(8,128)(2,1)}) fusion(bf16[2048,768]{0,1:T(8,128)(2,1)} %copy-done.7, bf16[2048,768]{0,1:T(8,128)(2,1)} %fusion.78, bf16[2,768,2304]{2,1,0:T(8,128)(2,1)} %param.14, bf16[2048,2304]{1,0:T(8,128)(2,1)} %convolution_convert_fusion.1, f32[2048,2304]{1,0:T(8,128)} %get-tuple-element.29), kind=kOutput, calls=%fused_computation.78 | convolution fusion | flops 7285504000 | bytes 41295872 | tf_op jit(solution)/shard_map/transpose(jvp())/dot_general | solution.py:22
  192.6 0.0 slice-start
  192.6 5.2 fusion.86
  197.8 0.0 slice-start.1
  197.8 11.6 %fusion.51 = bf16[1,2304,768]{2,1,0:T(8,128)(2,1)} fusion(bf16[2048,2304]{1,0:T(8,128)(2,1)} %get-tuple-element.24, bf16[2048,768]{0,1:T(8,128)(2,1)S(1)} %fusion.86), kind=kOutput, calls=%fused_computation.88 | convolution fusion | flops 7249526784 | bytes 16121856 | tf_op jit(solution)/shard_map/transpose(jvp())/dot_general | solution.py:10
  209.5 10.2 %convolution_convert_fusion = bf16[2048,2304]{1,0:T(8,128)(2,1)} fusion(bf16[2048,768]{0,1:T(8,128)(2,1)S(1)} %fusion.86, bf16[2,2304,768]{2,1,0:T(8,128)(2,1)S(1)} %bitcast.81), kind=kOutput, calls=%fused_computation.58 | convolution fusion | flops 7252475904 | bytes 16121856 | tf_op jit(solution)/shard_map/transpose(jvp())/dot_general | solution.py:10
  219.7 15.6 %fusion.52 = bf16[1,768,2304]{2,1,0:T(8,128)(2,1)} fusion(bf16[2048,2304]{1,0:T(8,128)(2,1)} %convolution_convert_fusion, f32[2048,2304]{1,0:T(8,128)} %fusion.70, bf16[1,2048,768]{1,2,0:T(8,128)(2,1)S(1)} %copy-done.3, f32[2048]{0:T(1024)S(1)} %copy-done.12), kind=kOutput, calls=%fused_computation.89 | convolution fusion | flops 7282556928 | bytes 35004416 | tf_op jit(solution)/shard_map/transpose(jvp())/dot_general | solution.py:22
  235.3 20.4 %fusion.53 = bf16[1,768,2304]{2,1,0:T(8,128)(2,1)} fusion(f32[2048,2304]{1,0:T(8,128)} %fusion.70, f32[2048,2304]{1,0:T(8,128)} %get-tuple-element.25, bf16[2048,2304]{1,0:T(8,128)(2,1)} %convolution_convert_fusion, bf16[1,2048,768]{1,2,0:T(8,128)(2,1)S(1)} %copy-done.3, f32[2048]{0:T(1024)S(1)} %copy-done.12), kind=kOutput, calls=%fused_computation.90 | convolution fusion | flops 7306149888 | bytes 53878784 | tf_op jit(solution)/shard_map/transpose(jvp())/dot_general | solution.py:21
  255.7 0.1 all-reduce.3.cloned.1.call-update
  255.8 258.3 %all-reduce.3.cloned.1.call-done = (bf16[1,768,2304]{2,1,0:T(8,128)(2,1)}, bf16[1,768,2304]{2,1,0:T(8,128)(2,1)}, bf16[1,768,2304]{2,1,0:T(8,128)(2,1)}, bf16[1,...) async-done(((bf16[1,768,2304]{2,1,0:T(8,128)(2,1)}, bf16[1,768,2304]{2,1,0:T(8,128)(2,1)}, bf16[1,768,2304]{2,1,0:T(8,128)(2,1)}, ...) | async-done | bytes 21233680 | tf_op jit(solution)/shard_map/psum | solution.py:50
  514.1 7.5 %fusion.22 = f32[]{:T(128)} fusion(bf16[1,2304,768]{2,1,0:T(8,128)(2,1)} %get-tuple-element.13, bf16[1,2304,768]{2,1,0:T(8,128)(2,1)} %get-tuple-element.14), kind=kLoop, calls=%fused_computation.46 | loop fusion | flops 14155775 | bytes 7077892 | tf_op jit(solution)/shard_map/reduce_sum | solution.py:52
  521.5 7.3 %fusion.21 = f32[]{:T(128)} fusion(bf16[1,768,2304]{2,1,0:T(8,128)(2,1)} %get-tuple-element.11, bf16[1,768,2304]{2,1,0:T(8,128)(2,1)} %get-tuple-element.12), kind=kLoop, calls=%fused_computation.45 | loop fusion | flops 14155775 | bytes 7077892 | tf_op jit(solution)/shard_map/reduce_sum | solution.py:52
  528.9 4.2 fusion.20
  535.1 24.8 %fusion.28 = (bf16[2,2304,768]{2,1,0:T(8,128)(2,1)}, f32[2,2304,768]{2,1,0:T(8,128)}, f32[2,2304,768]{2,1,0:T(8,128)}) fusion(bf16[2,2304,768]{2,1,0:T(8,128)(2,1)} %param.15, f32[]{:T(128)S(6)} %min_shard_map.3, bf16[1,2304,768]{2,1,0:T(8,128)(2,1)} %get-tuple-element.13, bf16[1,2304,768]{2,1,0:T(8,128)(2,1)} %get-tuple-element.14, ...), kind=kLoop, calls=%fused_computation.52 | loop fusion | flops 70778880 | bytes 77856768 | tf_op jit(solution)/shard_map/convert_element_type | solution.py:30
  559.9 47.5 %fusion.19 = (bf16[2,768,2304]{2,1,0:T(8,128)(2,1)}, f32[2,768,2304]{2,1,0:T(8,128)}, f32[2,768,2304]{2,1,0:T(8,128)}, bf16[2,768,2304]{2,1,0:T(8,128)(2,1)}, f3...) fusion(bf16[2,768,2304]{2,1,0:T(8,128)(2,1)} %param.13, f32[]{:T(128)S(6)} %min_shard_map.3, ...), kind=kLoop, calls=%fused_computation.43 | loop fusion | flops 141557760 | bytes 155713536 | tf_op jit(solution)/shard_map/convert_element_type | solution.py:30
  (36 shorter events, 0.1 us)
Async XLA Ops:
  7.2 506.9 %all-reduce.3.cloned.1.call-start = ((), (), s32[]{:S(2)}) async-start(), calls=%async_computation | async-start | bytes 42467328 | tf_op jit(solution)/shard_map/psum | solution.py:50
  10.5 50.2 %copy-start.2 = (bf16[1,2048,768]{1,2,0:T(8,128)(2,1)}, bf16[1,2048,768]{1,2,0:T(8,128)(2,1)S(1)}, u32[]{:S(2)}) copy-start(bf16[1,2048,768]{1,2,0:T(8,128)(2,1)S(1)} %copy.20) | copy-start | bytes 9437188
  11.1 30.6 %copy-start.11 = (f32[2048]{0:T(1024)}, f32[2048]{0:T(1024)S(1)}, u32[]{:S(2)}) copy-start(f32[2048]{0:T(1024)S(1)} %add_rsqrt_fusion) | copy-start | bytes 24580
  16.2 12.6 %copy-start.5 = (bf16[1,2048,768]{2,1,0:T(8,128)(2,1)S(1)}, bf16[1,2048,768]{2,1,0:T(8,128)(2,1)}, u32[]{:S(2)}) copy-start(bf16[1,2048,768]{2,1,0:T(8,128)(2,1)} %param.11) | copy-start | bytes 9437188
  72.5 0.6 copy-start.9
  72.6 1.7 copy-start.7
  74.2 44.1 %slice-start.2 = ((s8[7077888]{0:T(1024)(128)(4,1)}), s8[4194304]{0:T(1024)(128)(4,1)S(1)}, s32[]{:S(2)}) async-start(s8[7077888]{0:T(1024)(128)(4,1)} %bitcast.82), calls=%async_computation.3 | async-start | bytes 8388608
  87.8 30.5 %slice-start.3 = ((s8[7077888]{0:T(1024)(128)(4,1)}), s8[2883584]{0:T(1024)(128)(4,1)S(1)}, s32[]{:S(2)}) async-start(s8[7077888]{0:T(1024)(128)(4,1)} %bitcast.82), calls=%async_computation.4 | async-start | bytes 5767168
  118.3 11.4 %copy-start.8 = (bf16[2048,768]{0,1:T(8,128)(2,1)S(1)}, bf16[2048,768]{0,1:T(8,128)(2,1)}, u32[]{:S(2)}) copy-start(bf16[2048,768]{0,1:T(8,128)(2,1)} %copy-done.7) | copy-start | bytes 9437188
  118.3 11.3 %copy-start.13 = (bf16[2048,2304]{1,0:T(8,128)(2,1)S(1)}, bf16[2048,2304]{1,0:T(8,128)(2,1)}, u32[]{:S(2)}) copy-start(bf16[2048,2304]{1,0:T(8,128)(2,1)} %get-tuple-element.28) | copy-start | bytes 28311556
  129.7 8.9 %copy-start.6 = (bf16[1,2048,768]{2,1,0:T(8,128)(2,1)S(1)}, bf16[1,2048,768]{2,1,0:T(8,128)(2,1)}, u32[]{:S(2)}) copy-start(bf16[1,2048,768]{2,1,0:T(8,128)(2,1)} %param.12) | copy-start | bytes 9437188
  173.0 19.6 %copy-start.10 = (f32[2048]{0:T(1024)S(1)}, f32[2048]{0:T(1024)}, u32[]{:S(2)}) copy-start(f32[2048]{0:T(1024)} %copy-done.9) | copy-start | bytes 24580
  173.0 19.6 %copy-start.4 = (bf16[1,2048,768]{1,2,0:T(8,128)(2,1)S(1)}, bf16[1,2048,768]{1,2,0:T(8,128)(2,1)}, u32[]{:S(2)}) copy-start(bf16[1,2048,768]{1,2,0:T(8,128)(2,1)} %copy.21) | copy-start | bytes 9437188
  192.6 16.8 %slice-start = ((s8[7077888]{0:T(1024)(128)(4,1)}), s8[4194304]{0:T(1024)(128)(4,1)S(1)}, s32[]{:S(2)}) async-start(s8[7077888]{0:T(1024)(128)(4,1)} %bitcast.80), calls=%async_computation.1 | async-start | bytes 8388608
  197.8 11.6 %slice-start.1 = ((s8[7077888]{0:T(1024)(128)(4,1)}), s8[2883584]{0:T(1024)(128)(4,1)S(1)}, s32[]{:S(2)}) async-start(s8[7077888]{0:T(1024)(128)(4,1)} %bitcast.80), calls=%async_computation.2 | async-start | bytes 5767168
  209.4 10.2 %copy-start.3 = (bf16[1,2048,768]{1,2,0:T(8,128)(2,1)S(1)}, bf16[1,2048,768]{1,2,0:T(8,128)(2,1)}, u32[]{:S(2)}) copy-start(bf16[1,2048,768]{1,2,0:T(8,128)(2,1)} %copy-done.2) | copy-start | bytes 9437188
  209.4 10.2 %copy-start.12 = (f32[2048]{0:T(1024)S(1)}, f32[2048]{0:T(1024)}, u32[]{:S(2)}) copy-start(f32[2048]{0:T(1024)} %copy-done.11) | copy-start | bytes 24580
  514.1 14.8 %copy-start = (bf16[1,768,2304]{2,1,0:T(8,128)(2,1)S(1)}, bf16[1,768,2304]{2,1,0:T(8,128)(2,1)}, u32[]{:S(2)}) copy-start(bf16[1,768,2304]{2,1,0:T(8,128)(2,1)} %get-tuple-element.9) | copy-start | bytes 10616836
  514.1 14.8 %copy-start.1 = (bf16[1,768,2304]{2,1,0:T(8,128)(2,1)S(1)}, bf16[1,768,2304]{2,1,0:T(8,128)(2,1)}, u32[]{:S(2)}) copy-start(bf16[1,768,2304]{2,1,0:T(8,128)(2,1)} %get-tuple-element.10) | copy-start | bytes 10616836
Sparse Core Ops, SparseCore 0:
  255.9 258.1 all-reduce.2
where the time goes:
time: 622 us; the launch traced here: 615 us
  waiting for transfers between devices  258 us (41%)
  matrix products  232 us (37%)
  other arithmetic  97.2 us (16%)
  between operations  16.7 us (3%)
  local copies, waits for them, and re-layouts  9.94 us (2%)
    psum x1, waiting for transfers between devices, step(): summed[number] = [lax.psum(by_w[name], 'dp') for name in NAMES]  258 us
    dot_general x5, matrix products, layer(): gate = jnp.dot(a, w['w_gate'], preferred_element_type=jnp.float32)  84.2 us
    dot_general x5, matrix products, layer(): up = jnp.dot(a, w['w_up'], preferred_element_type=jnp.float32)  84 us
    convert_element_type x2, other arithmetic, adamw(): return ((w - 0.02 * step).astype(jnp.bfloat16), m, v)  72.3 us
    dot_general x5, matrix products, matmul(): jnp.dot(a, w, preferred_element_type=jnp.float32).astype(jnp.bfloat16)  64.2 us
    reduce_sum x3, other arithmetic, step(): jnp.sum(g * g)  19 us
  transfers between devices with their start and end apart: 1, of which 1 were waited for; matrix products, arithmetic and copies ran while one was open for 0% of the time, Pallas kernels for 0%

commit v1 on v0

v1 whole, which is shorter than its diff:
```python
import functools
import math

import jax
import jax.numpy as jnp
from jax import lax
from jax.experimental import pallas as pl
from jax.experimental.pallas import tpu as pltpu
from jax.sharding import PartitionSpec as P

MESH = pl.DeviceIdType.MESH
F32, BF16 = jnp.float32, jnp.bfloat16
BLOCK = 256
ROWS = 256
LANES = 128
OWN_SLOTS, RECV_SLOTS, SEND_SLOTS, KEEP_SLOTS, PUT_SLOTS = 8, 3, 2, 4, 4
COLOURS = ((0, 1), (0, -1), (1, 1), (1, -1))


def dot(a, b):
    return jnp.dot(a, b, preferred_element_type=F32)


def dot_t(a, b):
    return lax.dot_general(a, b, (((1,), (1,)), ((), ())), preferred_element_type=F32)


def step_kernel(dims, x_ref, dy_ref, wg_ref, wu_ref, wd_ref, shard_ref, square_ref, whole_ref,
                squares, h, a, a_t, ct, ct_t, acc, wg, wu, wd, p_gate, p_up, p_prod, own, r1, r2, s1, s2, keep,
                w_sem, io_sem, send_sem, recv_sem, put_sem, square_send, square_recv):
    side, gathered, layers, tokens, d, ff = dims
    blocks = ff // BLOCK
    units = layers * blocks
    forward = (layers - 1) * blocks
    unit_rows = own.shape[1]
    colour_rows = unit_rows // len(COLOURS)
    chunk, sub = colour_rows // side, colour_rows // (side * side)
    hops = side - 1
    steps = 2 * hops

    me = lax.axis_index("dp")
    place = (me // side, me % side)

    def neighbour(axis, by):
        at = list(place)
        at[axis] = lax.rem(at[axis] + by + side, side)
        return {"dp": at[0] * side + at[1]}

    peers = side * side
    barrier = pltpu.get_barrier_semaphore()
    for away in range(1, peers):
        pl.semaphore_signal(barrier, inc=1, device_id={"dp": lax.rem(me + away, peers)}, device_id_type=MESH)

    def weights(n):
        slot = lax.rem(n, 2)
        back = n - forward
        layer = jnp.where(n < forward, n // blocks, layers - 1 - back // blocks)
        at = pl.ds(pl.multiple_of(lax.rem(n, blocks) * BLOCK, BLOCK), BLOCK)
        return [
            pltpu.make_async_copy(wg_ref.at[layer, :, at], wg.at[slot], w_sem.at[slot, 0]),
            pltpu.make_async_copy(wu_ref.at[layer, :, at], wu.at[slot], w_sem.at[slot, 1]),
            pltpu.make_async_copy(wd_ref.at[layer, at, :], wd.at[slot], w_sem.at[slot, 2]),
        ]

    def next_weights(n):
        for copy in weights(n):
            copy.wait()

        @pl.when(n + 1 < forward + units)
        def _():
            for copy in weights(n + 1):
                copy.start()

    load_x, load_dy = (pltpu.make_async_copy(ref.at[0], ct, io_sem.at[i]) for i, ref in enumerate((x_ref, dy_ref)))
    load_x.start()
    for copy in weights(0):
        copy.start()

    tiles = [slice(at, at + ROWS) for at in range(0, tokens, ROWS)]

    def into(layer, rows):
        return ct[rows] if layer == 0 else h[layer - 1, rows]

    def norm_of(layer, rows):
        wide = into(layer, rows).astype(F32)
        scale = lax.rsqrt(jnp.mean(wide * wide, -1, keepdims=True) + 1e-6)
        return wide, scale

    def norm(layer):
        for rows in tiles:
            wide, scale = norm_of(layer, rows)
            out = (wide * scale).astype(BF16)
            a[layer, rows] = out
            a_t[layer, :, rows] = out.T

    load_x.wait()
    norm(0)

    for layer in range(layers - 1):
        acc[...] = jnp.zeros_like(acc)

        def forward_block(j, _, layer=layer):
            n = layer * blocks + j
            next_weights(n)
            slot = lax.rem(n, 2)
            for rows in tiles:
                at = a[layer, rows]
                gate, up = dot(at, wg[slot]), dot(at, wu[slot])
                prod = (gate * jax.nn.sigmoid(gate) * up).astype(BF16)
                acc[rows] += dot(prod, wd[slot])
            return 0

        lax.fori_loop(0, blocks, forward_block, 0)
        for rows in tiles:
            h[layer, rows] = into(layer, rows) + acc[rows].astype(BF16)
        if layer == 0:
            load_dy.start()
        norm(layer + 1)
    load_dy.wait()
    for rows in tiles:
        ct_t[:, rows] = ct[rows].T

    def copy_of(k, s, c, source):
        first, by = COLOURS[c]
        axis = first if s < hops else 1 - first
        slot = lax.rem(k, RECV_SLOTS)
        target = r1.at[slot, c, s] if s < hops else r2.at[slot, c, s - hops]
        return pltpu.make_async_remote_copy(
            src_ref=source, dst_ref=target, send_sem=send_sem.at[lax.rem(k, SEND_SLOTS), c, s],
            recv_sem=recv_sem.at[slot, c, s], device_id=neighbour(axis, by), device_id_type=MESH)

    def own_rows(c, s):
        first, by = COLOURS[c]
        q = lax.rem(place[first] - by * (1 + s) + 2 * side, side)
        return pl.ds(pl.multiple_of(c * colour_rows + q * chunk, chunk), chunk)

    def sub_at(c, t):
        first, by = COLOURS[c]
        return lax.rem(place[1 - first] - by * (1 + t) + 2 * side, side)

    def source_of(k, s, c):
        if s == 0:
            return own.at[lax.rem(k - 1, OWN_SLOTS), own_rows(c, 0)]
        if s < hops:
            return s1.at[lax.rem(k, SEND_SLOTS), c, s - 1]
        return s2.at[lax.rem(k, SEND_SLOTS), c, s - hops]

    def spread_rows(c, s):
        first, by = COLOURS[c]
        if s < hops:
            q, r = place[first], lax.rem(place[1 - first] - by * s + side, side)
            return pl.ds(pl.multiple_of(c * colour_rows + q * chunk + r * sub, 8), sub)
        q = lax.rem(place[first] - by * (s - hops) + side, side)
        return pl.ds(pl.multiple_of(c * colour_rows + q * chunk, chunk), chunk)

    def spread(k, s, c, p):
        first, by = COLOURS[c]
        axis = 1 - first if s < hops else first
        target = whole_ref.at[p, spread_rows(c, s)]
        return pltpu.make_async_remote_copy(
            src_ref=shard_ref.at[p, c] if s == 0 else target, dst_ref=target,
            send_sem=send_sem.at[lax.rem(k, SEND_SLOTS), c, steps + s], recv_sem=recv_sem.at[lax.rem(k, RECV_SLOTS), c, steps + s],
            device_id=neighbour(axis, by), device_id_type=MESH)

    def put(c, p):
        return pltpu.make_async_copy(shard_ref.at[p, c], whole_ref.at[p, spread_rows(c, 0)], put_sem.at[lax.rem(p, PUT_SLOTS), c])

    def within(p, last):
        return (p >= 0) & (p < last)

    def gather_step(k, s):
        p = k - 1 - steps - s
        safe = jnp.clip(p, 0, units - 1)
        if s < steps:
            @pl.when(within(p - SEND_SLOTS, gathered))
            def _():
                for c in range(len(COLOURS)):
                    spread(k, s, c, jnp.clip(p - SEND_SLOTS, 0, units - 1)).wait_send()

        @pl.when(within(p, gathered))
        def _():
            for c in range(len(COLOURS)):
                if s >= 1:
                    spread(k + RECV_SLOTS - 1, s - 1, c, safe).wait_recv()
                if s == hops:
                    put(c, safe).wait()
                if s < steps:
                    spread(k, s, c, safe).start()
                if s == 0:
                    put(c, safe).start()

    def sum_step(k, s):
        was, now = lax.rem(k + RECV_SLOTS - 1, RECV_SLOTS), lax.rem(k, SEND_SLOTS)
        p = k - 1 - s
        if s < steps:
            @pl.when(within(p - SEND_SLOTS, units))
            def _():
                for c in range(len(COLOURS)):
                    copy_of(k, s, c, source_of(k, s, c)).wait_send()

        @pl.when(within(p, units))
        def _():
            mine, kept = lax.rem(p + 2 * OWN_SLOTS, OWN_SLOTS), lax.rem(p + 2 * KEEP_SLOTS, KEEP_SLOTS)
            for c in range(len(COLOURS)):
                if s >= 1:
                    copy_of(k + RECV_SLOTS - 1, s - 1, c, source_of(k, s - 1, c)).wait_recv()
                if 1 <= s < hops:
                    s1[now, c, s - 1] = (r1[was, c, s - 1].astype(F32) + own[mine, own_rows(c, s)].astype(F32)).astype(BF16)
                elif s == hops:
                    total = r1[was, c, s - 1].astype(F32) + own[mine, own_rows(c, s)].astype(F32)
                    for i in range(side):
                        keep[kept, c, i] = total[i * sub : (i + 1) * sub]
                    s2[now, c, 0] = keep[kept, c, sub_at(c, 0)].astype(BF16)
                elif hops < s < steps:
                    t = s - hops
                    s2[now, c, t] = (r2[was, c, t - 1].astype(F32) + keep[kept, c, sub_at(c, t)]).astype(BF16)
                elif s == steps:
                    total = (r2[was, c, hops - 1].astype(F32) + keep[kept, c, sub_at(c, hops)]).astype(BF16)
                    shard_ref[p, c] = total
                    wide = total.astype(F32)
                    squares[me] += jnp.sum((wide * wide).reshape(sub // 8, 8, LANES), 0)
            if s < steps:
                for c in range(len(COLOURS)):
                    copy_of(k, s, c, source_of(k, s, c)).start()

    def communicate(k):
        for s in range(steps, 0, -1):
            gather_step(k, s)
        sum_step(k, steps)
        gather_step(k, 0)
        for s in range(steps - 1, -1, -1):
            sum_step(k, s)

    squares[me] = jnp.zeros((8, LANES), F32)
    pl.semaphore_wait(barrier, peers - 1)

    for back in range(layers):
        layer = layers - 1 - back
        if layer > 0:
            acc[...] = jnp.zeros_like(acc)

        def unit(j, _, layer=layer, back=back):
            k = back * blocks + j
            communicate(k)
            next_weights(forward + k)
            slot, mine = lax.rem(forward + k, 2), lax.rem(k, OWN_SLOTS)
            for rows in tiles:
                at = a[layer, rows]
                gate, up = dot(at, wg[slot]), dot(at, wu[slot])
                by_prod = dot_t(ct[rows], wd[slot]).astype(BF16).astype(F32)
                sig = jax.nn.sigmoid(gate)
                silu = gate * sig
                p_prod[rows] = (silu * up).astype(BF16)
                p_up[rows] = (by_prod * silu).astype(BF16)
                p_gate[rows] = (by_prod * up * (sig + silu * (1 - sig))).astype(BF16)
            at = 0
            for which in (p_gate, p_up):
                g = dot(a_t[layer], which[...]).astype(BF16)
                for i in range(BLOCK // LANES):
                    own[mine, at : at + d] = g[:, i * LANES : (i + 1) * LANES]
                    at += d
            g = dot(ct_t[...], p_prod[...]).astype(BF16).T
            for i in range(d // LANES):
                own[mine, at : at + BLOCK] = g[:, i * LANES : (i + 1) * LANES]
                at += BLOCK
            if layer > 0:
                for rows in tiles:
                    acc[rows] += dot_t(p_gate[rows], wg[slot]) + dot_t(p_up[rows], wu[slot])
            return 0

        lax.fori_loop(0, blocks, unit, 0)
        if layer > 0:
            for rows in tiles:
                wide, scale = norm_of(layer, rows)
                by_a = acc[rows].astype(BF16).astype(F32)
                by_h = by_a * scale - wide * (scale * scale * scale * jnp.mean(by_a * wide, -1, keepdims=True))
                new = ct[rows] + by_h.astype(BF16)
                ct[rows] = new
                ct_t[:, rows] = new.T

    def drain(k, _):
        communicate(k)
        return 0

    done = units + steps + 1
    lax.fori_loop(units, done, drain, 0)

    def square_to(away):
        return pltpu.make_async_remote_copy(
            src_ref=squares.at[me], dst_ref=squares.at[me], send_sem=square_send.at[away], recv_sem=square_recv.at[me],
            device_id={"dp": lax.rem(me + away, peers)}, device_id_type=MESH)

    for away in range(1, peers):
        square_to(away).start()
    lax.fori_loop(done, max(done + 1, gathered + 2 * steps + 2), drain, 0)
    for away in range(1, peers):
        square_to(away).wait_send()
        other = lax.rem(me + away, peers)
        pltpu.make_async_remote_copy(
            src_ref=squares.at[other], dst_ref=squares.at[other], send_sem=square_send.at[away], recv_sem=square_recv.at[other],
            device_id={"dp": other}, device_id_type=MESH).wait_recv()
    total = squares[0]
    for i in range(1, peers):
        total = total + squares[i]
    square_ref[...] = total


def gradients(n, gathered, x, dy, w_gate, w_up, w_down):
    side = math.isqrt(n)
    layers, d, ff = w_gate.shape
    tokens = x.shape[1]
    units, unit_rows = layers * (ff // BLOCK), 3 * d * BLOCK // LANES
    colours = len(COLOURS)
    chunk, sub = unit_rows // (colours * side), unit_rows // (colours * side * side)
    hops = side - 1
    dims = (side, gathered, layers, tokens, d, ff)
    any_space, vmem = pl.BlockSpec(memory_space=pl.ANY), pl.BlockSpec(memory_space=pltpu.VMEM)
    return pl.pallas_call(
        functools.partial(step_kernel, dims),
        out_shape=(
            jax.ShapeDtypeStruct((units, colours, sub, LANES), BF16),
            jax.ShapeDtypeStruct((8, LANES), F32),
            jax.ShapeDtypeStruct((gathered, unit_rows, LANES), BF16),
        ),
        in_specs=[any_space] * 5,
        out_specs=(vmem, vmem, any_space),
        scratch_shapes=[
            pltpu.VMEM((n, 8, LANES), F32),
            pltpu.VMEM((layers - 1, tokens, d), BF16),
            pltpu.VMEM((layers, tokens, d), BF16),
            pltpu.VMEM((layers, d, tokens), BF16),
            pltpu.VMEM((tokens, d), BF16),
            pltpu.VMEM((d, tokens), BF16),
            pltpu.VMEM((tokens, d), F32),
            pltpu.VMEM((2, d, BLOCK), BF16),
            pltpu.VMEM((2, d, BLOCK), BF16),
            pltpu.VMEM((2, BLOCK, d), BF16),
            pltpu.VMEM((tokens, BLOCK), BF16),
            pltpu.VMEM((tokens, BLOCK), BF16),
            pltpu.VMEM((tokens, BLOCK), BF16),
            pltpu.VMEM((OWN_SLOTS, unit_rows, LANES), BF16),
            pltpu.VMEM((RECV_SLOTS, colours, hops, chunk, LANES), BF16),
            pltpu.VMEM((RECV_SLOTS, colours, hops, sub, LANES), BF16),
            pltpu.VMEM((SEND_SLOTS, colours, hops - 1, chunk, LANES), BF16),
            pltpu.VMEM((SEND_SLOTS, colours, hops, sub, LANES), BF16),
            pltpu.VMEM((KEEP_SLOTS, colours, side, sub, LANES), F32),
            pltpu.SemaphoreType.DMA((2, 3)),
            pltpu.SemaphoreType.DMA((2,)),
            pltpu.SemaphoreType.DMA((SEND_SLOTS, colours, 4 * hops)),
            pltpu.SemaphoreType.DMA((RECV_SLOTS, colours, 4 * hops)),
            pltpu.SemaphoreType.DMA((PUT_SLOTS, colours)),
            pltpu.SemaphoreType.DMA((n,)),
            pltpu.SemaphoreType.DMA((n,)),
        ],
        compiler_params=pltpu.CompilerParams(collective_id=0, has_side_effects=True, vmem_limit_bytes=67043328),
    )(x, dy, w_gate, w_up, w_down)


def update_kernel(runs, factor_ref, g_ref, *refs):
    ins, outs = refs[:9], refs[9:]
    factor = factor_ref[0, 0]
    for which, rows, cols, at in runs:
        g = g_ref[0, at].astype(F32) * factor
        m = 0.9 * ins[3 + which][0, rows, cols] + 0.1 * g
        v = 0.95 * ins[6 + which][0, rows, cols] + 0.05 * g * g
        w = ins[which][0, rows, cols].astype(F32)
        outs[which][0, rows, cols] = (w - 0.02 * (m * lax.rsqrt(v + 1e-8) + 0.1 * w)).astype(BF16)
        outs[3 + which][0, rows, cols] = m
        outs[6 + which][0, rows, cols] = v


def update(factor, g, arrays):
    layers, d, ff = arrays[0].shape
    blocks = ff // BLOCK
    runs, at = [], 0
    for which, height, width in ((0, d, BLOCK), (1, d, BLOCK), (2, BLOCK, d)):
        for i in range(width // LANES):
            for top in range(0, height, 64):
                runs.append((which, slice(top, top + 64), slice(i * LANES, (i + 1) * LANES), slice(at, at + 64)))
                at += 64

    def wide(u):
        return layers - 1 - u // blocks, 0, u % blocks

    def tall(u):
        return layers - 1 - u // blocks, u % blocks, 0

    specs = [pl.BlockSpec((1, d, BLOCK), wide), pl.BlockSpec((1, d, BLOCK), wide), pl.BlockSpec((1, BLOCK, d), tall)] * 3
    return pl.pallas_call(
        functools.partial(update_kernel, runs),
        grid=(layers * blocks,),
        out_shape=tuple(jax.ShapeDtypeStruct(a.shape, a.dtype) for a in arrays),
        in_specs=[pl.BlockSpec(memory_space=pltpu.SMEM), pl.BlockSpec((1, g.shape[1], LANES), lambda u: (u, 0, 0))] + specs,
        out_specs=tuple(specs),
        compiler_params=pltpu.CompilerParams(vmem_limit_bytes=50 * 2**20),
    )(factor, g, *arrays)


def solution(mesh):
    n = mesh.shape["dp"]

    def step(x, dy, *arrays):
        layers, d, ff = arrays[0].shape
        units = layers * (ff // BLOCK)
        shards, squares, whole = gradients(n, units, x, dy, *arrays[:3])
        count = sum(w.size for w in arrays[:3])
        factor = jnp.minimum(1.0, 0.5 * lax.rsqrt(jnp.sum(squares) / count + 1e-30))
        return update(factor.reshape(1, 1), whole, arrays)

    return jax.shard_map(
        step,
        mesh=mesh,
        in_specs=(P(("rep", "dp"), None, None),) * 2 + (P(None, None, None),) * 9,
        out_specs=(P("rep", None, None),) * 9,
        check_vma=False,
    )
```

time: 622 us -> 383 us (0.62)
  Pallas kernels: 0 us -> 379 us
  waiting for transfers between devices: 258 us -> 0 us
  matrix products: 232 us -> 0 us
  other arithmetic: 97.2 us -> 1.29 us
  between operations: 16.7 us -> 1.52 us
  local copies, waits for them, and re-layouts: 9.94 us -> 0 us
    pallas_call x0 -> x2, Pallas kernels: none -> 379 us  [the longest x1 301 us: gradients(): pl.pallas_call(functools.partial(step_kernel, dims), out_shape=(jax.Shape...]
    psum x1 -> x0, waiting for transfers between devices: 258 us -> none  [step(): summed[number] = [lax.psum(by_w[name], 'dp') for name in NAMES]]
    dot_general x15 -> x0, matrix products: 232 us -> none  [the longest x5 84.2 us: layer(): gate = jnp.dot(a, w['w_gate'], preferred_element_type=jnp.float32)]
    convert_element_type x2 -> x0, other arithmetic: 72.3 us -> none  [adamw(): return ((w - 0.02 * step).astype(jnp.bfloat16), m, v)]
    reduce_sum x4 -> x1, other arithmetic: 19.7 us -> 1.29 us  [step(): factor = jnp.minimum(1.0, 0.5 * lax.rsqrt(jnp.sum(squares) / count + 1e-30))]
    unnamed x38 -> x0, local copies, waits for them, and re-layouts: 9.94 us -> none
  transfers between devices with their start and end apart: 1 -> 0, of which waited for: 1 -> 0; matrix products, arithmetic and copies ran while one was open for 0% -> 0% of each run, Pallas kernels for 0% -> 0%
where the time goes in v1:
time: 383 us; the launch traced here: 382 us
  Pallas kernels  379 us (99%)
    pallas_call x1, Pallas kernels, gradients(): pl.pallas_call(functools.partial(step_kernel, dims), out_shape=(jax.Shape...  301 us
    pallas_call x1, Pallas kernels, update(): pl.pallas_call(functools.partial(update_kernel, runs), grid=(layers * blo...  77.8 us

profile of v1, /device:TPU:97, one launch (start us, length us, event | category | flops | bytes accessed | tf_op | source)
XLA Modules:
  0.0 381.6 jit_solution(3383094815037467467)
XLA Ops:
  0.6 301.0 %shard_map.178 = (bf16[18,4,72,128]{3,2,1,0:T(8,128)(2,1)}, f32[8,128]{1,0:T(8,128)}, bf16[18,4608,128]{2,1,0:T(8,128)(2,1)}) custom-call(bf16[1,2048,768]{2,1,0:T(8,128)(2,1)} %x_ref.1, bf16[1,2048,768]{2,1,0:T(8,128)(2,1)} %dy_ref.1, bf16[2,768,2304]{2,1,0:T(8,128)(2,1)} %refs_0_.1, bf16[2,768,2304]{2,1,0:T(8,128)(2,1)} %refs_1_.1, ...), custom_call_target="tpu_custom_call" | custom-call | tf_op jit(solution)/shard_map/pallas_call | solution.py:318
  301.6 1.3 reduce_sum.9
  303.6 77.8 %shard_map.179 = (bf16[2,768,2304]{2,1,0:T(8,128)(2,1)}, bf16[2,768,2304]{2,1,0:T(8,128)(2,1)}, bf16[2,2304,768]{2,1,0:T(8,128)(2,1)}, f32[2,768,2304]{2,1,0:T(8...) custom-call(f32[1,1]{1,0:T(1,128)} %bitcast.factor_ref, ...), custom_call_target="tpu_custom_call" | custom-call | tf_op jit(solution)/shard_map/pallas_call | solution.py:389
